TPU v7x, 256 devices: a whole 4x4x8 slice. The times are simulated.
256 devices in a mesh: ctx: 32 (over y, x, core), head: 8 (over z).
Axes of the slice: x: 4, y: 4, z: 8, core: 2. Of those that a mesh axis runs over, the one named last changes fastest.
Arguments:
- query_in: float32 [32768, 16, 128], P('ctx', 'head'), may hold values from -6 to 6
- key_in: float32 [32768, 16, 128], P('ctx', 'head'), may hold values from -6 to 6
- value_in: float32 [32768, 32, 128], P('ctx', 'head'), may hold values from -6 to 6
- gate_in: float32 [32768, 32, 128], P('ctx', 'head'), may hold values from -6 to 6
- log_gate: float32 [32, 32768], P('head', 'ctx'), may hold values from -1 to 0, as said below
- strength: float32 [32, 32768], P('head', 'ctx'), may hold values from 0.005 to 0.05
- query_conv: float32 [4, 16, 128], P(None, 'head'), may hold values from -3 to 3
- key_conv: float32 [4, 16, 128], P(None, 'head'), may hold values from -3 to 3
- value_conv: float32 [4, 32, 128], P(None, 'head'), may hold values from -3 to 3
- norm_gain: float32 [128], replicated, may hold values from 0.1 to 1.9
- out_weight: bfloat16 [4096, 2048], P('head'), may hold values from -0.09375 to 0.09375
Outputs:
- mixed: float32 [32768, 2048], P(('ctx', 'head'))
Inputs may be any that keep to these rules, and one draw needn't show every extreme that they name: `log_gate`: the logarithm of head h's decay factor at a token.
All inputs are finite; a program needn't handle non-finite values.
Results may differ from a plain program's by a relative error of at most 0.015.
Values may be sent and summed in bfloat16 or wider, within the bound.
No kernel may reach another device: no remote copies, remote signals or barrier semaphores. Data moves between devices by JAX's collectives and lax.ppermute only.
A program may use at most 128 MiB of HBM per device.

v0:
```python
import jax
import jax.numpy as jnp
from jax import lax
from jax.sharding import Mesh
from jax.sharding import PartitionSpec as P

SPAN = 64
CTX = ("ctx_0", "ctx_1", "ctx_2")
CTX_HEAD = ("ctx_0", "ctx_1", "ctx_2", "head")


norm_epsilon = 1e-06


def from_behind(value, axis, steps):
    count = lax.axis_size(axis)
    initial, last = (max(0, -steps), min(count, count - steps))
    return lax.ppermute(value, axis, [(source, source + steps) for source in range(initial, last)])


def neutral_like(x, identity):
    return jax.tree.map(
        lambda part, zero: jnp.zeros_like(part) + jnp.asarray(zero, part.dtype), x, identity
    )


def entering_2(x, axes, combine, identity):
    before = start = neutral_like(x, identity)
    total = x
    for axis in reversed(axes):
        length, here = (lax.axis_size(axis), lax.axis_index(axis))
        pieces = jax.tree.map(
            lambda part, kind: lax.all_gather(part.astype(kind), axis),
            total,
            (jnp.bfloat16, jnp.bfloat16),
        )
        inside, total = (start, start)
        for k in range(length):
            passed = k < here
            total = combine(
                total, jax.tree.map(lambda part, own: part[k].astype(own.dtype), pieces, x)
            )
            inside = jax.tree.map(lambda new, old: jnp.where(passed, new, old), total, inside)
        before = combine(inside, before)
    return before


def causal_mix(current, previous, kernel):
    kernel_width = kernel.shape[0]
    token_count = current.shape[0]
    padded = jnp.concatenate([previous, current], axis=0)
    summed = jnp.zeros(current.shape, jnp.float32)
    for offset in range(kernel_width):
        summed = summed + kernel[offset] * padded[offset : offset + token_count]
    return jax.nn.silu(summed)


def unit_rows(matrix):
    return matrix * lax.rsqrt(jnp.sum(matrix * matrix, axis=-1, keepdims=True) + norm_epsilon)


def to_blocks(matrix, block_size):
    token_count, head_count, width_count = matrix.shape
    return matrix.reshape(token_count // block_size, block_size, head_count, width_count).transpose(
        0, 2, 1, 3
    )


def gate_blocks(matrix, block_size):
    head_count, token_count = matrix.shape
    return matrix.reshape(head_count, token_count // block_size, block_size).transpose(1, 0, 2)


def prepare(
    query_in,
    key_in,
    value_in,
    query_prev,
    key_prev,
    value_prev,
    query_conv,
    key_conv,
    value_conv,
    block_size,
):
    group_ratio = value_in.shape[1] // query_in.shape[1]
    queries = unit_rows(causal_mix(query_in, query_prev, query_conv)) * query_in.shape[2] ** (-0.5)
    key_rows = unit_rows(causal_mix(key_in, key_prev, key_conv))
    values = causal_mix(value_in, value_prev, value_conv)
    queries = jnp.repeat(queries, group_ratio, axis=1)
    key_rows = jnp.repeat(key_rows, group_ratio, axis=1)
    return (
        to_blocks(queries, block_size),
        to_blocks(key_rows, block_size),
        to_blocks(values, block_size),
    )


def unit_inverse(mixing):
    block_size = mixing.shape[-1]
    identity_map = jnp.eye(block_size, dtype=jnp.float32)
    powered = -mixing
    inverse = identity_map + powered
    reach = 2
    while reach < block_size:
        powered = jnp.einsum("nhij,nhjk->nhik", powered, powered)
        inverse = jnp.einsum("nhij,nhjk->nhik", inverse, identity_map + powered)
        reach = reach * 2
    return inverse


def span_setup(queries, key_rows, values, log_gate, strength):
    cumulative = jnp.cumsum(log_gate, axis=-1)
    block_size = cumulative.shape[-1]
    row_index = lax.broadcasted_iota(jnp.int32, (block_size, block_size), 0)
    col_index = lax.broadcasted_iota(jnp.int32, (block_size, block_size), 1)
    lower_mask = row_index >= col_index
    strict_mask = row_index > col_index
    differences = cumulative[..., :, None] - cumulative[..., None, :]
    decay_table = jnp.exp(jnp.where(lower_mask, differences, -jnp.inf))
    key_inner = jnp.einsum("nhcd,nhmd->nhcm", key_rows, key_rows)
    mixing = jnp.where(strict_mask, strength[..., :, None] * key_inner * decay_table, 0.0)
    scores = jnp.where(
        lower_mask, jnp.einsum("nhcd,nhmd->nhcm", queries, key_rows) * decay_table, 0.0
    )
    inverse = unit_inverse(mixing)
    fresh_values = jnp.einsum("nhcm,nhmw->nhcw", inverse, strength[..., None] * values)
    solved_keys = jnp.einsum(
        "nhcm,nhmd->nhcd", inverse, (strength * jnp.exp(cumulative))[..., None] * key_rows
    )
    lifted = jnp.exp(cumulative)[..., None] * queries
    carried = jnp.exp(cumulative[..., -1:] - cumulative)[..., None] * key_rows
    ending = jnp.exp(cumulative[..., -1])
    return (fresh_values, solved_keys, scores, lifted, carried, ending)


def run_spans(start_state, setup):

    def advance(carry_state, per_span):
        fresh_block, solved_block, score_block, lifted_block, carried_block, ending_block = per_span
        update = fresh_block - jnp.einsum("hcd,hdw->hcw", solved_block, carry_state)
        new_state = ending_block[:, None, None] * carry_state + jnp.einsum(
            "hcd,hcw->hdw", carried_block, update
        )
        result = jnp.einsum("hcd,hdw->hcw", lifted_block, carry_state)
        result = result + jnp.einsum("hcm,hmw->hcw", score_block, update)
        return (new_state, result)

    return lax.scan(advance, start_state, setup)


def gated_norm(recurrent, gate_in, norm_gain):
    scaled = recurrent * lax.rsqrt(
        jnp.mean(recurrent * recurrent, axis=-1, keepdims=True) + norm_epsilon
    )
    return scaled * norm_gain * jax.nn.silu(gate_in)


def batched(left, right):
    return jnp.einsum("hij,hjk->hik", left, right)


def compose_maps(earlier, latter):
    return (batched(latter[0], earlier[0]), batched(latter[0], earlier[1]) + latter[1])


def on_device(
    query_in,
    key_in,
    value_in,
    gate_in,
    log_gate,
    strength,
    query_conv,
    key_conv,
    value_conv,
    norm_gain,
    out_weight,
):
    rim_count = query_conv.shape[0] - 1
    query_prev, key_prev, value_prev = from_behind(
        (query_in[-rim_count:], key_in[-rim_count:], value_in[-rim_count:]), CTX, 1
    )
    queries, key_rows, values = prepare(
        query_in,
        key_in,
        value_in,
        query_prev,
        key_prev,
        value_prev,
        query_conv,
        key_conv,
        value_conv,
        SPAN,
    )
    setup = span_setup(
        queries, key_rows, values, gate_blocks(log_gate, SPAN), gate_blocks(strength, SPAN)
    )
    fresh_values, solved_keys, scores, lifted, carried, ending = setup
    token_count = query_in.shape[0]
    head_dev = values.shape[1]
    key_width = key_rows.shape[3]
    value_width = values.shape[3]
    identity_map = jnp.broadcast_to(
        jnp.eye(key_width, dtype=jnp.float32), (head_dev, key_width, key_width)
    )
    empty_state = jnp.zeros((head_dev, key_width, value_width), jnp.float32)
    start_state = jnp.concatenate([identity_map, empty_state], axis=2)
    widened = jnp.concatenate([jnp.zeros(key_rows.shape, jnp.float32), fresh_values], axis=3)
    widened_setup = (widened, solved_keys, scores, lifted, carried, ending)
    final_state, widened_out = run_spans(start_state, widened_setup)
    transition = final_state[:, :, :key_width]
    offset = final_state[:, :, key_width:]
    scanned = entering_2((transition, offset), CTX, compose_maps, (identity_map, empty_state))
    entering = scanned[1]
    recurrent = widened_out[..., key_width:] + jnp.einsum(
        "nhcd,hdw->nhcw", widened_out[..., :key_width], entering
    )
    recurrent = recurrent.transpose(0, 2, 1, 3).reshape(token_count, head_dev, value_width)
    normed = (
        gated_norm(recurrent, gate_in, norm_gain)
        .astype(jnp.bfloat16)
        .reshape(token_count, head_dev * value_width)
    )
    return lax.psum_scatter(
        jnp.dot(normed, out_weight, preferred_element_type=jnp.float32).astype(jnp.bfloat16),
        "head",
        scatter_dimension=0,
        tiled=True,
    ).astype(jnp.float32)


def solution(mesh):
    split = Mesh(
        mesh.devices.reshape(4, 4, 2, mesh.shape["head"]), ("ctx_0", "ctx_1", "ctx_2", "head")
    )
    in_specs = (
        P(CTX, "head", None),
        P(CTX, "head", None),
        P(CTX, "head", None),
        P(CTX, "head", None),
        P("head", CTX),
        P("head", CTX),
        P(None, "head", None),
        P(None, "head", None),
        P(None, "head", None),
        P(),
        P("head", None),
    )
    out_specs = P(CTX_HEAD, None)
    return jax.shard_map(
        on_device, mesh=split, in_specs=in_specs, out_specs=out_specs, check_vma=False
    )
```

profile of v0, /device:TPU:1, one launch (start us, length us, event | category | flops | bytes accessed | tf_op | source)
XLA Modules:
  0.0 301.1 jit_solution(17357008909973411985)
XLA Ops:
  7.4 4.5 %collective-permute-start = (f32[3,2,128]{2,1,0:T(2,128)S(1)}, f32[3,2,128]{2,1,0:T(2,128)S(1)}, u32[]{:S(2)}, u32[]{:S(2)}) collective-permute-start(f32[3,2,128]{2,1,0:T(2,128)S(1)} %slice.152), channel_id=1, source_target_pairs={{0,8},{8,16},{16,24},{24,32},{32,40},{40,48},{48,56},{56,64},{64,7... | collective-permute-start | bytes 9224 | tf_op jit(solution)/shard_map/ppermute | solution.py:18
  15.2 3.5 %collective-permute-start.1 = (f32[3,4,128]{2,1,0:T(4,128)S(1)}, f32[3,4,128]{2,1,0:T(4,128)S(1)}, u32[]{:S(2)}, u32[]{:S(2)}) collective-permute-start(f32[3,4,128]{2,1,0:T(4,128)S(1)} %slice.160), channel_id=1, source_target_pairs={{0,8},{8,16},{16,24},{24,32},{32,40},{40,48},{48,56},{56,64},{64,7... | collective-permute-start | bytes 18440 | tf_op jit(solution)/shard_map/ppermute | solution.py:18
  25.4 2.6 multiply_reduce_fusion.1
  28.1 2.4 broadcast_multiply_fusion.3
  38.3 4.5 %fusion.36 = bf16[16,4,64,64]{3,2,1,0:T(8,128)(2,1)} fusion(f32[16,4,64,64]{3,2,1,0:T(8,128)} %copy-done.2, f32[16,4,64,64]{3,2,1,0:T(8,128)} %copy-done.1, f32[16,4,64,64]{3,2,1,0:T(8,128)} %copy-done.3, f32[64,64]{1,0:T(8,128)S(1)} %fusion.135), kind=kOutput, calls=%fused_computation.51 | convolution fusion | flops 67895296 | bytes 3686400 | tf_op jit(solution)/shard_map/nhij,nhjk->nhik/dot_general | solution.py:107
  42.8 4.0 %fusion.151 = f32[16,4,64,64]{3,2,1,0:T(8,128)} fusion(f32[16,4,64,64]{3,2,1,0:T(8,128)} %fusion.150), kind=kOutput, calls=%fused_computation.184 | convolution fusion | flops 33554432 | bytes 2097152 | tf_op jit(solution)/shard_map/nhij,nhjk->nhik/dot_general | solution.py:106
  46.8 4.2 %fusion.32 = bf16[16,4,64,64]{3,2,1,0:T(8,128)(2,1)} fusion(f32[16,4,64,64]{3,2,1,0:T(8,128)} %fusion.151, bf16[16,4,64,64]{3,2,1,0:T(8,128)(2,1)} %fusion.36, f32[16,4,64,64]{3,2,1,0:T(8,128)} %fusion.150, f32[64,64]{1,0:T(8,128)S(1)} %fusion.135), kind=kOutput, calls=%fused_computation.47 | convolution fusion | flops 67633152 | bytes 3162112 | tf_op jit(solution)/shard_map/nhij,nhjk->nhik/dot_general | solution.py:107
  51.1 4.2 %fusion.30 = bf16[16,4,64,64]{3,2,1,0:T(8,128)(2,1)} fusion(bf16[16,4,64,64]{3,2,1,0:T(8,128)(2,1)} %fusion.32, f32[16,4,64,64]{3,2,1,0:T(8,128)} %fusion.151, f32[64,64]{1,0:T(8,128)S(1)} %fusion.135), kind=kOutput, calls=%fused_computation.45 | convolution fusion | flops 67633152 | bytes 2113536 | tf_op jit(solution)/shard_map/nhij,nhjk->nhik/dot_general | solution.py:107
  56.9 2.6 multiply_reduce_fusion
  59.5 2.4 multiply_multiply_fusion
  65.3 3.0 %broadcast_multiply_fusion.1 = (bf16[16,4,64,128]{3,2,0,1:T(8,128)(2,1)S(1)}, bf16[16,4,64,128]{3,2,0,1:T(8,128)(2,1)}, bf16[16,4,64,128]{3,2,0,1:T(8,128)(2,1)}) fusion(f32[16,4,64,128]{3,2,0,1:T(8,128)S(1)} %bitcast.157, f32[16,4,64]{2,0,1:T(8,128)S(1)} %get-tuple-element.109, f32[16,4,64]{2,0,1:T(8,128)S(1)} %get-tuple-element.110, ...), kind=kLoop, calls=%fused_computation.98 | loop fusion | flops 3145728 | bytes 7389184 | tf_op jit(solution)/shard_map/mul | solution.py:129
  73.4 2.5 concatenate.18
  76.0 82.2 %while.12 = (s32[]{:T(128)}, f32[4,128,256]{2,1,0:T(8,128)S(1)}, f32[16,4,64,256]{3,2,0,1:T(8,128)}, f32[16,4]{1,0:T(8,128)S(1)}, bf16[16,4,64,128]{3,2,0,1:T(8,...) while((s32[]{:T(128)}, f32[4,128,256]{2,1,0:T(8,128)S(1)}, ...), condition=%wide.region_4.5_spmd, body=%wide.region_3.4_spmd.sunk | while | flops 59179008 | bytes 3804313 | solution.py:149
  158.2 2.0 all-gather
  160.6 2.0 all-gather.3
  162.9 11.1 %all-gather.4 = bf16[16,128,128]{2,1,0:T(8,128)(2,1)S(1)} all-gather(bf16[4,128,128]{2,1,0:T(8,128)(2,1)S(1)} %convolution_add_fusion.8), channel_id=6, replica_groups=mesh['ctx_0'=4,'ctx_1'=4,'ctx_2'=2,'head'=8] {'ctx_1'}, dimensions={0}, use_global_device_ids=true | all-gather | bytes 655360 | tf_op jit(solution)/shard_map/all_gather | solution.py:33
  174.0 9.9 %all-gather.1 = bf16[16,128,128]{2,1,0:T(8,128)(2,1)S(1)} all-gather(bf16[4,128,128]{2,1,0:T(8,128)(2,1)S(1)} %fusion.152), channel_id=3, replica_groups=mesh['ctx_0'=4,'ctx_1'=4,'ctx_2'=2,'head'=8] {'ctx_1'}, dimensions={0}, use_global_device_ids=true | all-gather | bytes 655360 | tf_op jit(solution)/shard_map/all_gather | solution.py:33
  184.8 10.2 %all-gather.5 = bf16[16,128,128]{2,1,0:T(8,128)(2,1)S(1)} all-gather(bf16[4,128,128]{2,1,0:T(8,128)(2,1)S(1)} %convolution_add_fusion.5), channel_id=7, replica_groups=mesh['ctx_0'=4,'ctx_1'=4,'ctx_2'=2,'head'=8] {'ctx_0'}, dimensions={0}, use_global_device_ids=true | all-gather | bytes 655360 | tf_op jit(solution)/shard_map/all_gather | solution.py:33
  195.5 11.4 %all-gather.2 = bf16[16,128,128]{2,1,0:T(8,128)(2,1)S(1)} all-gather(bf16[4,128,128]{2,1,0:T(8,128)(2,1)S(1)} %fusion.155), channel_id=4, replica_groups=mesh['ctx_0'=4,'ctx_1'=4,'ctx_2'=2,'head'=8] {'ctx_0'}, dimensions={0}, use_global_device_ids=true | all-gather | bytes 655360 | tf_op jit(solution)/shard_map/all_gather | solution.py:33
  209.9 4.4 %fusion.20 = (f32[16,64,4]{1,0,2:T(8,128)S(1)}, f32[16,4,64,128]{3,2,0,1:T(8,128)}) fusion(f32[16,4,64,256]{3,2,0,1:T(8,128)} %get-tuple-element.53, f32[4,128,128]{2,1,0:T(8,128)S(1)} %fusion.63, f32[4,128,128]{2,1,0:T(8,128)S(1)} %fusion.85, bf16[4,128,128]{2,1,0:T(8,128)(2,1)S(1)} %convolution_add_fusion.8, bf16[4,128,128]{2,1,0:T(8,128)(2,1)} %copy-done.10, ...), kind=kOutput, calls=%fused_computation.31 | convolution fusion | flops 152891392 | bytes 7159810 | tf_op jit(solution)/shard_map/nhcd,hdw->nhcw/dot_general | solution.py:216
  214.6 7.5 %fusion.45 = bf16[1024,4,128]{2,1,0:T(4,128)(2,1)S(1)} fusion(f32[1024,4,128]{2,1,0:T(4,128)} %param.16, f32[1024,4,128]{2,0,1:T(8,128)} %bitcast.158, f32[128]{0:T(128)S(1)} %copy-done.11, f32[1024,4]{1,0:T(8,128)S(1)} %bitcast.162), kind=kLoop, calls=%fused_computation.58 | loop fusion | flops 4194304 | bytes 5259776 | tf_op jit(solution)/shard_map/convert_element_type | solution.py:222
  222.1 4.3 %convolution_convert_fusion = bf16[1024,2048]{1,0:T(8,128)(2,1)} fusion(bf16[512,2048]{1,0:T(8,128)(2,1)S(1)} %copy-done, bf16[128,8,4,128]{3,2,1,0:T(4,128)(2,1)S(1)} %bitcast.163), kind=kOutput, calls=%fused_computation.20 | convolution fusion | flops 2149580800 | bytes 7340032 | tf_op jit(solution)/shard_map/dot_general | solution.py:226
  226.4 65.8 %reduce-scatter.2.cloned.1.call-done = bf16[128,2048]{1,0:T(8,128)(2,1)} async-done(((bf16[1024,2048]{1,0:T(8,128)(2,1)}), bf16[128,2048]{1,0:T(8,128)(2,1)}) %reduce-scatter.2.cloned.1.call-update) | async-done | bytes 524304 | tf_op jit(solution)/shard_map/reduce_scatter | solution.py:225
  292.2 2.1 convert_element_type.153
  (174 shorter events, 115.5 us)
Async XLA Ops:
  6.5 215.5 %copy-start = (bf16[512,2048]{1,0:T(8,128)(2,1)S(1)}, bf16[512,2048]{1,0:T(8,128)(2,1)}, u32[]{:S(2)}) copy-start(bf16[512,2048]{1,0:T(8,128)(2,1)} %param.23) | copy-start | bytes 6291460
  6.5 285.6 %reduce-scatter.2.cloned.1.call-start = ((), (), s32[]{:S(2)}) async-start(), calls=%async_computation.1 | async-start | bytes 4718592 | tf_op jit(solution)/shard_map/reduce_scatter | solution.py:225
  7.4 16.5 %collective-permute-start = (f32[3,2,128]{2,1,0:T(2,128)S(1)}, f32[3,2,128]{2,1,0:T(2,128)S(1)}, u32[]{:S(2)}, u32[]{:S(2)}) collective-permute-start(f32[3,2,128]{2,1,0:T(2,128)S(1)} %slice.152), channel_id=1, source_target_pairs={{0,8},{8,16},{16,24},{24,32},{32,40},{40,48},{48,56},{56,64},{64,7... | collective-permute-start | bytes 9224 | tf_op jit(solution)/shard_map/ppermute | solution.py:18
  12.6 42.8 %collective-permute-start.2 = (f32[3,2,128]{2,1,0:T(2,128)S(1)}, f32[3,2,128]{2,1,0:T(2,128)S(1)}, u32[]{:S(2)}, u32[]{:S(2)}) collective-permute-start(f32[3,2,128]{2,1,0:T(2,128)S(1)} %slice.168), channel_id=1, source_target_pairs={{0,8},{8,16},{16,24},{24,32},{32,40},{40,48},{48,56},{56,64},{64,7... | collective-permute-start | bytes 9224 | tf_op jit(solution)/shard_map/ppermute | solution.py:18
  15.2 54.6 %collective-permute-start.1 = (f32[3,4,128]{2,1,0:T(4,128)S(1)}, f32[3,4,128]{2,1,0:T(4,128)S(1)}, u32[]{:S(2)}, u32[]{:S(2)}) collective-permute-start(f32[3,4,128]{2,1,0:T(4,128)S(1)} %slice.160), channel_id=1, source_target_pairs={{0,8},{8,16},{16,24},{24,32},{32,40},{40,48},{48,56},{56,64},{64,7... | collective-permute-start | bytes 18440 | tf_op jit(solution)/shard_map/ppermute | solution.py:18
  23.9 1.5 copy-start.8
  30.7 1.3 copy-start.6
  32.1 1.3 copy-start.3
  33.8 1.3 copy-start.1
  35.1 1.4 copy-start.2
  55.3 1.5 copy-start.9
  62.0 1.6 copy-start.7
  65.3 3.0 %copy-start.4 = (bf16[16,4,64,64]{3,2,1,0:T(8,128)(2,1)S(1)}, bf16[16,4,64,64]{3,2,1,0:T(8,128)(2,1)}, u32[]{:S(2)}) copy-start(bf16[16,4,64,64]{3,2,1,0:T(8,128)(2,1)} %fusion.30) | copy-start | bytes 1572868
  68.3 2.0 copy-start.5
  162.7 21.9 %copy-start.10 = (bf16[4,128,128]{2,1,0:T(8,128)(2,1)}, bf16[4,128,128]{2,1,0:T(8,128)(2,1)S(1)}, u32[]{:S(2)}) copy-start(bf16[4,128,128]{2,1,0:T(8,128)(2,1)S(1)} %convolution_add_fusion.9) | copy-start | bytes 393220
  209.9 4.7 %copy-start.11 = (f32[128]{0:T(128)S(1)}, f32[128]{0:T(128)}, u32[]{:S(2)}) copy-start(f32[128]{0:T(128)} %param.22) | copy-start | bytes 1540
Sparse Core Ops, SparseCore 0:
  226.5 65.6 reduce-scatter.1
where the time goes:
time: 304 us; the launch traced here: 301 us
  matrix products  120 us (39%)
  waiting for transfers between devices  65.8 us (22%)
  blocking collectives  46.5 us (15%)
  other arithmetic  25.6 us (8%)
  local copies, waits for them, and re-layouts  18.7 us (6%)
  between operations  13.9 us (5%)
  starting transfers between devices  9.89 us (3%)
    reduce_scatter x1, waiting for transfers between devices, on_device(): lax.psum_scatter(jnp.dot(normed, out_weight, preferred_element_type=jnp.f...  65.8 us
    all_gather x6, blocking collectives, entering_2(): lax.all_gather(part.astype(kind), axis)  46.5 us
    dot_general x16, matrix products, advance(): result = result + jnp.einsum('hcm,hmw->hcw', score_block, update)  27.4 us
    dot_general x16, matrix products, advance(): jnp.einsum('hcd,hcw->hdw', carried_block, update)  19 us
    dot_general x16, matrix products, advance(): update = fresh_block - jnp.einsum('hcd,hdw->hcw', solved_block, carry_state)  18.7 us
    dot_general x16, matrix products, advance(): result = jnp.einsum('hcd,hdw->hcw', lifted_block, carry_state)  16.3 us
    dot_general x3, matrix products, unit_inverse(): inverse = jnp.einsum('nhij,nhjk->nhik', inverse, identity_map + powered)  13 us
    ppermute x3, starting transfers between devices, from_behind(): lax.ppermute(value, axis, [(source, source + steps) for source in range(i...  9.88 us
  transfers between devices with their start and end apart: 4, of which 1 were waited for; matrix products, arithmetic and copies ran while one was open for 16% of the time, Pallas kernels for 0%

commit v1 on v0

v1 whole, which is shorter than its diff:
```python
import functools
import jax
import jax.numpy as jnp
from jax import lax
from jax.experimental import pallas as pl
from jax.experimental.pallas import tpu as pltpu
from jax.sharding import Mesh
from jax.sharding import PartitionSpec as P

CTX = ("ctx_0", "ctx_1", "ctx_2")
CTX_HEAD = ("ctx_0", "ctx_1", "ctx_2", "head")
CHUNK = 128
WIDTH = 128
PAD = 8
GROUP = 4
norm_epsilon = 1e-06
f32 = jnp.float32
bf16 = jnp.bfloat16


def mm(left, right):
    return jnp.dot(left, right, preferred_element_type=f32)


def silu(u):
    half = 0.5 * u
    return half + half * jnp.tanh(half)


def paired(x):
    zero = jnp.zeros((CHUNK, CHUNK), x.dtype)
    top = jnp.concatenate([x[:, :CHUNK], zero], axis=1)
    low = jnp.concatenate([zero, x[:, CHUNK:]], axis=1)
    return jnp.concatenate([top, low], axis=0)


def local_kernel(
    q_hbm, k_hbm, v_hbm, rim_ref, qw_ref, kw_ref, vw_ref, gate_ref,
    low_ref, wide_ref, state_ref,
    q_pad, k_pad, v_pad, solved_ref, fresh_ref, read_ref, write_ref, end_ref, mask_ref, sems,
):
    chunks = gate_ref.shape[0]
    qheads = qw_ref.shape[1]
    vheads = vw_ref.shape[1]
    blocks = chunks // GROUP
    streams = ((q_hbm, q_pad, qheads), (k_hbm, k_pad, qheads), (v_hbm, v_pad, vheads))

    def copy(which, block):
        source, target, heads = streams[which]
        rows = GROUP * CHUNK * heads
        return pltpu.make_async_copy(
            source.at[pl.ds(block * rows, rows), :],
            target.at[pl.ds(PAD * heads + block * rows, rows), :],
            sems.at[which, block],
        )

    for block in range(blocks):
        for which in range(3):
            copy(which, block).start()
    first = 0
    for which in range(3):
        _, target, heads = streams[which]
        for step in range(3):
            target[pl.ds((PAD - 3 + step) * heads, heads), :] = rim_ref[step, first : first + heads, :]
        first += heads

    row = lax.broadcasted_iota(jnp.int32, (CHUNK, 2 * CHUNK), 0)
    col = lax.broadcasted_iota(jnp.int32, (CHUNK, 2 * CHUNK), 1) & (CHUNK - 1)

    def same(bits):
        return (row >> bits) == (col >> bits)

    mask_ref[0] = same(4).astype(bf16)
    for level in range(3):
        mask_ref[1 + level] = (same(5 + level) & jnp.logical_not(same(4 + level))).astype(bf16)
    eye2 = (row == col).astype(f32)
    row1 = lax.broadcasted_iota(jnp.int32, (CHUNK, CHUNK), 0)
    col1 = lax.broadcasted_iota(jnp.int32, (CHUNK, CHUNK), 1)
    lower = row1 >= col1
    strict = row1 > col1
    adder = (row1 <= col1).astype(bf16)

    def mix(target, weight_ref, heads, head, start):
        total = None
        for tap in range(4):
            piece = target[pl.ds((start + PAD - 3 + tap) * heads + head, CHUNK, stride=heads), :]
            part = weight_ref[tap, head : head + 1, :] * piece
            total = part if total is None else total + part
        return silu(total)

    def unit(x):
        return x * lax.rsqrt(jnp.sum(x * x, axis=1, keepdims=True) + norm_epsilon)

    def setup(block):
        units = []
        for inner in range(GROUP):
            chunk = block * GROUP + inner
            start = chunk * CHUNK
            gates = gate_ref[chunk]
            hi = gates.astype(bf16).astype(f32)
            rest = gates - hi
            mid = rest.astype(bf16).astype(f32)
            parts = jnp.concatenate([hi, mid, rest - mid], axis=0).astype(bf16)
            sums = mm(parts, adder)
            running = sums[0:8] + sums[8:16] + sums[16:24]
            both = jnp.concatenate([running[0:4], gates[4:8]], axis=0)
            columns = both.T
            end_row = running[:, CHUNK - 1 : CHUNK]
            tail_row = jnp.exp(end_row - running)
            end_ref[chunk] = jnp.broadcast_to(jnp.exp(end_row), (8, CHUNK))
            for g in range(qheads):
                query = unit(mix(q_pad, qw_ref, qheads, g, start)) * (WIDTH ** -0.5)
                key = unit(mix(k_pad, kw_ref, qheads, g, start))
                key_t = key.T
                inner_products = mm(
                    jnp.concatenate([key, query], axis=0).astype(bf16), key_t.astype(bf16)
                )
                kk, qk = inner_products[:CHUNK], inner_products[CHUNK:]
                mixing = []
                rights = []
                for side in range(vheads // qheads):
                    head = g * (vheads // qheads) + side
                    decay_col = jnp.broadcast_to(columns[:, head : head + 1], (CHUNK, CHUNK))
                    gain_col = jnp.broadcast_to(columns[:, 4 + head : 5 + head], (CHUNK, CHUNK))
                    table = jnp.where(
                        lower, jnp.exp(jnp.minimum(decay_col - running[head : head + 1, :], 0.0)), 0.0
                    )
                    lift = jnp.exp(decay_col)
                    mixing.append(jnp.where(strict, gain_col * kk * table, 0.0).astype(bf16))
                    value = mix(v_pad, vw_ref, vheads, head, start)
                    rights.append(
                        jnp.concatenate(
                            [(gain_col * lift * key).astype(bf16), (gain_col * value).astype(bf16)],
                            axis=1,
                        )
                    )
                    read_ref[chunk, head] = jnp.concatenate(
                        [(lift * query).astype(bf16), (qk * table).astype(bf16)], axis=1
                    )
                    write_ref[chunk, head] = (key_t * tail_row[head : head + 1, :]).astype(bf16)
                units.append((chunk, g, jnp.concatenate(mixing, axis=1), rights))
        mixings = [u[2] for u in units]
        powers = [m * mask_ref[0] for m in mixings]
        inverses = [eye2 - p.astype(f32) for p in powers]
        powers = [mm(p, paired(p)).astype(bf16) for p in powers]
        for step in range(3):
            grown = [mm(p, paired(x.astype(bf16))) for p, x in zip(powers, inverses)]
            if step < 2:
                powers = [mm(p, paired(p)).astype(bf16) for p in powers]
            inverses = [x + y for x, y in zip(inverses, grown)]
        for level in range(3):
            packed = [x.astype(bf16) for x in inverses]
            crossed = [mm(m * mask_ref[1 + level], paired(x)).astype(bf16) for m, x in zip(mixings, packed)]
            grown = [mm(x, paired(y)) for x, y in zip(packed, crossed)]
            inverses = [x - y for x, y in zip(inverses, grown)]
        for (chunk, g, _, rights), inverse in zip(units, inverses):
            packed = inverse.astype(bf16)
            for side, right in enumerate(rights):
                head = g * (vheads // qheads) + side
                answer = mm(packed[:, side * CHUNK : (side + 1) * CHUNK], right)
                solved_ref[chunk, head] = answer[:, :CHUNK].astype(bf16)
                fresh_ref[chunk, head] = answer[:, CHUNK:]

    def block_step(block, carry):
        for which in range(3):
            copy(which, block).wait()
        setup(block)
        return carry

    lax.fori_loop(0, blocks, block_step, 0)

    def chunk_step(chunk, states):
        packed = [s.astype(bf16) for s in states]
        taken = [mm(solved_ref[chunk, h], packed[h]) for h in range(vheads)]
        updates = [
            jnp.concatenate(
                [-taken[h][:, :WIDTH], fresh_ref[chunk, h] - taken[h][:, WIDTH:]], axis=1
            ).astype(bf16)
            for h in range(vheads)
        ]
        fresh_states = []
        ends = end_ref[chunk]
        for h in range(vheads):
            added = mm(write_ref[chunk, h], updates[h])
            end = ends[h : h + 1, :]
            fresh_states.append(states[h] * jnp.concatenate([end, end], axis=1) + added)
        for h in range(vheads):
            result = mm(read_ref[chunk, h], jnp.concatenate([packed[h], updates[h]], axis=0))
            rows = pl.ds(pl.multiple_of(chunk * CHUNK, CHUNK), CHUNK)
            wide_ref[h, rows, :] = result[:, :WIDTH].astype(bf16)
            low_ref[h, rows, :] = result[:, WIDTH:]
        return fresh_states

    begin = jnp.concatenate(
        [(row1 == col1).astype(f32), jnp.zeros((CHUNK, CHUNK), f32)], axis=1
    )
    states = lax.fori_loop(0, chunks, chunk_step, [begin] * vheads)
    for h in range(vheads):
        state_ref[h] = states[h].astype(bf16)


def local_call(query, key, value, rim, query_conv, key_conv, value_conv, gates, interpret=False):
    chunks = gates.shape[0]
    tokens = chunks * CHUNK
    qheads = query_conv.shape[1]
    vheads = value_conv.shape[1]
    anywhere = pl.BlockSpec(memory_space=pl.ANY)
    inside = pl.BlockSpec(memory_space=pltpu.VMEM)
    return pl.pallas_call(
        local_kernel,
        out_shape=(
            jax.ShapeDtypeStruct((vheads, tokens, WIDTH), f32),
            jax.ShapeDtypeStruct((vheads, tokens, WIDTH), bf16),
            jax.ShapeDtypeStruct((vheads, WIDTH, 2 * WIDTH), bf16),
        ),
        in_specs=[anywhere] * 3 + [inside] * 5,
        out_specs=(inside,) * 3,
        scratch_shapes=[
            pltpu.VMEM(((PAD + tokens) * qheads, WIDTH), f32),
            pltpu.VMEM(((PAD + tokens) * qheads, WIDTH), f32),
            pltpu.VMEM(((PAD + tokens) * vheads, WIDTH), f32),
            pltpu.VMEM((chunks, vheads, CHUNK, WIDTH), bf16),
            pltpu.VMEM((chunks, vheads, CHUNK, WIDTH), f32),
            pltpu.VMEM((chunks, vheads, CHUNK, 2 * CHUNK), bf16),
            pltpu.VMEM((chunks, vheads, CHUNK, CHUNK), bf16),
            pltpu.VMEM((chunks, 8, CHUNK), f32),
            pltpu.VMEM((4, CHUNK, 2 * CHUNK), bf16),
            pltpu.SemaphoreType.DMA((3, chunks // GROUP)),
        ],
        compiler_params=pltpu.CompilerParams(vmem_limit_bytes=40 * 1024 * 1024),
        interpret=interpret,
        name="local_map",
    )(
        query.reshape(tokens * qheads, WIDTH),
        key.reshape(tokens * qheads, WIDTH),
        value.reshape(tokens * vheads, WIDTH),
        rim, query_conv, key_conv, value_conv, gates,
    )


def total_kernel(place_ref, mine_ref, other_ref, total_ref, first_ref):
    core = place_ref[1]
    for h in range(mine_ref.shape[0]):
        mine, other = mine_ref[h], other_ref[h]
        first = jnp.where(core == 0, mine, other)
        second = jnp.where(core == 0, other, mine)
        joined = mm(second[:, :WIDTH], first)
        total_ref[h] = jnp.concatenate(
            [joined[:, :WIDTH], joined[:, WIDTH:] + second[:, WIDTH:].astype(f32)], axis=1
        ).astype(bf16)
        first_ref[h] = first


def prefix_kernel(place_ref, all_ref, first_ref, mine_ref, send_ref, held_ref):
    heads = first_ref.shape[0]
    core = place_ref[1]
    held_ref[...] = jnp.zeros_like(held_ref)

    def step(j, carry):
        for h in range(heads):
            moved = mm(all_ref[j, h, :, :WIDTH], held_ref[h])
            held_ref[h] = (moved + all_ref[j, h, :, WIDTH:].astype(f32)).astype(bf16)
        return carry

    lax.fori_loop(0, place_ref[0], step, 0)
    for h in range(heads):
        before = held_ref[h]
        after = mm(first_ref[h, :, :WIDTH], before) + first_ref[h, :, WIDTH:].astype(f32)
        wide = before.astype(f32)
        mine_ref[h] = jnp.where(core == 0, wide, after).astype(bf16)
        send_ref[h] = jnp.where(core == 0, after, wide).astype(bf16)


def output_kernel(place_ref, low_ref, wide_ref, near_ref, far_ref, gate_ref, gain_ref, weight_ref, out_ref):
    core = place_ref[1]
    heads = low_ref.shape[0]
    half = heads // 2
    rows = low_ref.shape[1]
    pieces = []
    for h in range(heads):
        entering = jnp.where(core == h // half, near_ref[h % half], far_ref[h % half])
        recurrent = low_ref[h] + mm(wide_ref[h], entering)
        scaled = recurrent * lax.rsqrt(
            jnp.mean(recurrent * recurrent, axis=1, keepdims=True) + norm_epsilon
        )
        gate = gate_ref[pl.ds(h, rows, stride=heads), :]
        pieces.append((scaled * gain_ref[...] * silu(gate)).astype(bf16))
    out_ref[...] = mm(jnp.concatenate(pieces, axis=1), weight_ref[...]).astype(bf16)


def output_call(place, low, wide, near, far, gate_in, norm_gain, out_weight, rows=256):
    heads, tokens, _ = low.shape
    model = out_weight.shape[1]
    scalar = pl.BlockSpec(memory_space=pltpu.SMEM)
    return pl.pallas_call(
        output_kernel,
        out_shape=jax.ShapeDtypeStruct((tokens, model), bf16),
        grid=(tokens // rows,),
        in_specs=[
            scalar,
            pl.BlockSpec((heads, rows, WIDTH), lambda i: (0, i, 0)),
            pl.BlockSpec((heads, rows, WIDTH), lambda i: (0, i, 0)),
            pl.BlockSpec(near.shape, lambda i: (0, 0, 0)),
            pl.BlockSpec(far.shape, lambda i: (0, 0, 0)),
            pl.BlockSpec((rows * heads, WIDTH), lambda i: (i, 0)),
            pl.BlockSpec((1, WIDTH), lambda i: (0, 0)),
            pl.BlockSpec(out_weight.shape, lambda i: (0, 0)),
        ],
        out_specs=pl.BlockSpec((rows, model), lambda i: (i, 0)),
        compiler_params=pltpu.CompilerParams(vmem_limit_bytes=32 * 1024 * 1024),
        name="gated_output",
    )(
        place, low, wide, near, far,
        gate_in.reshape(tokens * heads, WIDTH), norm_gain.reshape(1, WIDTH), out_weight,
    )


def on_device(
    query_in, key_in, value_in, gate_in, log_gate, strength,
    query_conv, key_conv, value_conv, norm_gain, out_weight,
):
    rim_count = query_conv.shape[0] - 1
    count = lax.axis_size(CTX)
    rim = jnp.concatenate(
        [query_in[-rim_count:], key_in[-rim_count:], value_in[-rim_count:]], axis=1
    )
    rim = lax.ppermute(rim, CTX, [(i, i + 1) for i in range(count - 1)])
    vheads, tokens = log_gate.shape
    gates = jnp.concatenate(
        [
            log_gate.reshape(vheads, tokens // CHUNK, CHUNK),
            strength.reshape(vheads, tokens // CHUNK, CHUNK),
        ],
        axis=0,
    ).transpose(1, 0, 2)
    low, wide, state = local_call(
        query_in, key_in, value_in, rim, query_conv, key_conv, value_conv, gates
    )
    core = lax.axis_index("ctx_2")
    chip = lax.axis_index(("ctx_0", "ctx_1"))
    place = jnp.stack([chip, core]).astype(jnp.int32)
    half = vheads // 2
    mine = lax.dynamic_slice_in_dim(state, core * half, half, axis=0)
    other = lax.dynamic_slice_in_dim(state, (1 - core) * half, half, axis=0)
    swap = [(0, 1), (1, 0)]
    other = lax.ppermute(other, "ctx_2", swap)
    scalar = pl.BlockSpec(memory_space=pltpu.SMEM)
    inside = pl.BlockSpec(memory_space=pltpu.VMEM)
    same = jax.ShapeDtypeStruct(mine.shape, bf16)
    total, first = pl.pallas_call(
        total_kernel,
        out_shape=(same, same),
        in_specs=[scalar, inside, inside],
        out_specs=(inside, inside),
        name="chip_total",
    )(place, mine, other)
    everyone = lax.all_gather(total, ("ctx_0", "ctx_1"))
    entering = jax.ShapeDtypeStruct((half, WIDTH, WIDTH), bf16)
    near, send = pl.pallas_call(
        prefix_kernel,
        out_shape=(entering, entering),
        in_specs=[scalar, inside, inside],
        out_specs=(inside, inside),
        scratch_shapes=[pltpu.VMEM((half, WIDTH, WIDTH), bf16)],
        name="prefix",
    )(place, everyone, first)
    far = lax.ppermute(send, "ctx_2", swap)
    partial = output_call(place, low, wide, near, far, gate_in, norm_gain, out_weight)
    return lax.psum_scatter(partial, "head", scatter_dimension=0, tiled=True).astype(f32)


def solution(mesh):
    split = Mesh(
        mesh.devices.reshape(4, 4, 2, mesh.shape["head"]), ("ctx_0", "ctx_1", "ctx_2", "head")
    )
    in_specs = (
        P(CTX, "head", None),
        P(CTX, "head", None),
        P(CTX, "head", None),
        P(CTX, "head", None),
        P("head", CTX),
        P("head", CTX),
        P(None, "head", None),
        P(None, "head", None),
        P(None, "head", None),
        P(),
        P("head", None),
    )
    return jax.shard_map(
        on_device, mesh=split, in_specs=in_specs, out_specs=P(CTX_HEAD, None), check_vma=False
    )
```

time: 304 us -> 174 us (0.57)
  matrix products: 120 us -> 0 us
  blocking collectives: 46.5 us -> 0 us
  waiting for transfers between devices: 65.8 us -> 110 us
  Pallas kernels: 0 us -> 22.7 us
  other arithmetic: 25.6 us -> 3.44 us
  starting transfers between devices: 9.89 us -> 6.76 us
    dot_general x96 -> x0, matrix products: 120 us -> none  [the longest x16 27.4 us: advance(): result = result + jnp.einsum('hcm,hmw->hcw', score_block, update)]
    all_gather x0 -> x1, waiting for transfers between devices: none -> 51.9 us  [on_device(): everyone = lax.all_gather(total, ('ctx_0', 'ctx_1'))]
    all_gather x6 -> x0, blocking collectives: 46.5 us -> none  [entering_2(): lax.all_gather(part.astype(kind), axis)]
    pallas_call x0 -> x4, Pallas kernels: none -> 22.7 us  [the longest x1 13.8 us: local_call(): pl.pallas_call(local_kernel, out_shape=(jax.ShapeDtypeStruct((vheads, tok...]
    mul x4 -> x0, other arithmetic: 9.74 us -> none  [the longest x1 3.03 us: span_setup(): (strength * jnp.exp(cumulative))[..., None] * key_rows]
    reduce_scatter x1, waiting for transfers between devices: 65.8 us -> 56.5 us  [on_device(): lax.psum_scatter(partial, 'head', scatter_dimension=0, tiled=True)]
    unnamed x27 -> x30, local copies, waits for them, and re-layouts: 5.89 us -> 14.1 us
    convert_element_type x4 -> x1, other arithmetic: 9.62 us -> 2.12 us  [on_device(): lax.psum_scatter(partial, 'head', scatter_dimension=0, tiled=True)]
  transfers between devices with their start and end apart: 4 -> 5, of which waited for: 1 -> 5; matrix products, arithmetic and copies ran while one was open for 16% -> 1% of each run, Pallas kernels for 0% -> 0%
where the time goes in v1:
time: 174 us
  waiting for transfers between devices  110 us (63%)
  Pallas kernels  22.7 us (13%)
  local copies, waits for them, and re-layouts  16.8 us (10%)
  between operations  13.5 us (8%)
  starting transfers between devices  6.76 us (4%)
  other arithmetic  3.44 us (2%)
    reduce_scatter x1, waiting for transfers between devices, on_device(): lax.psum_scatter(partial, 'head', scatter_dimension=0, tiled=True)  56.5 us
    all_gather x1, waiting for transfers between devices, on_device(): everyone = lax.all_gather(total, ('ctx_0', 'ctx_1'))  51.9 us
    unnamed x30, local copies, waits for them, and re-layouts  14.1 us
    pallas_call x1, Pallas kernels, local_call(): pl.pallas_call(local_kernel, out_shape=(jax.ShapeDtypeStruct((vheads, tok...  13.8 us
    pallas_call x1, Pallas kernels, output_call(): pl.pallas_call(output_kernel, out_shape=jax.ShapeDtypeStruct((tokens, mod...  4.75 us
    ppermute x1, starting transfers between devices, on_device(): rim = lax.ppermute(rim, CTX, [(i, i + 1) for i in range(count - 1)])  4.5 us
  transfers between devices with their start and end apart: 5, of which 5 were waited for; matrix products, arithmetic and copies ran while one was open for 1% of the time, Pallas kernels for 0%

profile of v1, /device:TPU:1, one launch (start us, length us, event | category | flops | bytes accessed | tf_op | source)
XLA Modules:
  0.0 173.6 jit_solution(13819277208957501553)
XLA Ops:
  6.5 0.7 slice.9
  7.2 0.7 slice.10
  7.9 0.7 slice.11
  8.6 4.5 %collective-permute-start = (f32[3,8,128]{2,1,0:T(8,128)S(1)}, f32[3,8,128]{2,1,0:T(8,128)S(1)}, u32[]{:S(2)}, u32[]{:S(2)}) collective-permute-start(f32[3,8,128]{2,1,0:T(8,128)S(1)} %pad_maximum_fusion), channel_id=1, source_target_pairs={{0,8},{8,16},{16,24},{24,32},{32,40},{40,48},{48,56},{56,64},{64,7... | collective-permute-start | bytes 36872 | tf_op jit(solution)/shard_map/ppermute | solution.py:327
  13.1 0.7 maximum_bitcast_fusion.gate_ref
  13.9 1.6 copy-done.1
  15.5 1.2 copy-done.6
  16.7 1.2 copy-done.7
  18.0 0.7 copy-done.9
  20.0 13.8 %local_map.1 = (f32[4,1024,128]{2,1,0:T(8,128)S(1)}, bf16[4,1024,128]{2,1,0:T(8,128)(2,1)S(1)}, bf16[4,128,256]{2,1,0:T(8,128)(2,1)S(1)}) custom-call(f32[2048,128]{1,0:T(8,128)S(1)} %bitcast.14, f32[2048,128]{1,0:T(8,128)S(1)} %bitcast.15, f32[4096,128]{1,0:T(8,128)S(1)} %bitcast.12, f32[3,8,128]{2,1,0:T(8,128)S(1)} %collective-permute-done.rim_ref, ...), custom_call_target="tpu_custom_call" | custom-call | tf_op jit(solution)/shard_map/local_map/pallas_call | solution.py:209
  33.8 1.3 copy-done.4
  36.4 0.8 collective-permute-done.1.other_ref
  37.8 1.8 %chip_total.1 = (bf16[2,128,256]{2,1,0:T(8,128)(2,1)}, bf16[2,128,256]{2,1,0:T(8,128)(2,1)}) custom-call(s32[2]{0:T(128)} %pad_add_fusion.place_ref, bf16[2,128,256]{2,1,0:T(8,128)(2,1)} %get-tuple-element.20.mine_ref, bf16[2,128,256]{2,1,0:T(8,128)(2,1)} %copy-done.14), custom_call_target="tpu_custom_call" | custom-call | tf_op jit(solution)/shard_map/chip_total/pallas_call | solution.py:350
  39.7 51.9 %all-gather.3.cloned.1.call-done = bf16[32,128,256]{2,1,0:T(8,128)(2,1)} async-done(((bf16[2,128,256]{2,1,0:T(8,128)(2,1)}), bf16[32,128,256]{2,1,0:T(8,128)(2,1)}) %all-gather.3.cloned.1.call-update) | async-done | bytes 2097168 | tf_op jit(solution)/shard_map/all_gather | solution.py:357
  91.7 2.4 %prefix.1 = (bf16[2,128,128]{2,1,0:T(8,128)(2,1)}, bf16[2,128,128]{2,1,0:T(8,128)(2,1)}) custom-call(s32[2]{0:T(128)} %pad_add_fusion.place_ref, bf16[16,2,128,256]{3,2,1,0:T(8,128)(2,1)} %bitcast.17, bf16[2,128,256]{2,1,0:T(8,128)(2,1)} %get-tuple-element.16.first_ref), custom_call_target="tpu_custom_call" | custom-call | tf_op jit(solution)/shard_map/prefix/pallas_call | solution.py:359
  94.1 2.2 %collective-permute-start.2 = (bf16[2,128,128]{2,1,0:T(8,128)(2,1)}, bf16[2,128,128]{2,1,0:T(8,128)(2,1)S(1)}, u32[]{:S(2)}, u32[]{:S(2)}) collective-permute-start(bf16[2,128,128]{2,1,0:T(8,128)(2,1)} %get-tuple-element.18), channel_id=1, source_target_pairs={{0,8},{8,0},{1,9},{9,1},{2,10},{10,2},{3,11},{11,3},{4,12},{12,4},... | collective-permute-start | bytes 196616 | tf_op jit(solution)/shard_map/ppermute | solution.py:367
  96.3 1.1 collective-permute-done.2.far_ref
  97.4 1.6 copy-done.3
  99.0 1.6 copy-done.5
  100.6 0.8 copy-done.8
  101.5 4.7 %gated_output.1 = bf16[1024,2048]{1,0:T(8,128)(2,1)S(1)} custom-call(s32[2]{0:T(128)S(1)} %copy-done.10, f32[4,1024,128]{2,1,0:T(8,128)S(1)} %copy-done.5, bf16[4,1024,128]{2,1,0:T(8,128)(2,1)S(1)} %get-tuple-element.13.wide_ref, bf16[2,128,128]{2,1,0:T(8,128)(2,1)S(1)} %copy-done.8, bf16[2,128,128]{2,1,0:T(8,128)(2,1)S(1)} %collective-permute-done.2.far_ref, ...), custom_call_target="tpu_custom_call" | custom-call | tf_op jit(solution)/shard_map/gated_output/pallas_call | solution.py:295
  106.2 1.9 %copy-done = bf16[1024,2048]{1,0:T(8,128)(2,1)} copy-done((bf16[1024,2048]{1,0:T(8,128)(2,1)}, bf16[1024,2048]{1,0:T(8,128)(2,1)S(1)}, u32[]{:S(2)}) %copy-start) | copy-done | bytes 4194328
  108.2 56.5 %reduce-scatter.2.cloned.1.call-done = bf16[128,2048]{1,0:T(8,128)(2,1)} async-done(((bf16[1024,2048]{1,0:T(8,128)(2,1)}), bf16[128,2048]{1,0:T(8,128)(2,1)}) %reduce-scatter.2.cloned.1.call-update) | async-done | bytes 524304 | tf_op jit(solution)/shard_map/reduce_scatter | solution.py:369
  164.7 2.1 %convert_element_type.3 = f32[128,2048]{1,0:T(8,128)} convert(bf16[128,2048]{1,0:T(8,128)(2,1)} %reduce-scatter.2.cloned.1.call-done) | non-fusion elementwise | flops 262144 | bytes 1572864 | tf_op jit(solution)/shard_map/convert_element_type | solution.py:369
  (30 shorter events, 3.4 us)
Async XLA Ops:
  6.5 85.1 %all-gather.3.cloned.1.call-start = ((), (), s32[]{:S(2)}) async-start(), calls=%async_computation.2 | async-start | bytes 2228224 | tf_op jit(solution)/shard_map/all_gather | solution.py:357
  8.6 5.3 %collective-permute-start = (f32[3,8,128]{2,1,0:T(8,128)S(1)}, f32[3,8,128]{2,1,0:T(8,128)S(1)}, u32[]{:S(2)}, u32[]{:S(2)}) collective-permute-start(f32[3,8,128]{2,1,0:T(8,128)S(1)} %pad_maximum_fusion), channel_id=1, source_target_pairs={{0,8},{8,16},{16,24},{24,32},{32,40},{40,48},{48,56},{56,64},{64,7... | collective-permute-start | bytes 36872 | tf_op jit(solution)/shard_map/ppermute | solution.py:327
  13.9 1.6 copy-start.1
  15.5 1.2 copy-start.6
  16.7 1.2 copy-start.7
  18.0 0.7 copy-start.9
  18.7 0.7 copy-start.11
  19.4 0.7 copy-start.12
  33.8 1.3 copy-start.4
  35.2 62.3 %copy-start.2 = (f32[1024,4,128]{2,1,0:T(4,128)S(1)}, f32[1024,4,128]{2,1,0:T(4,128)}, u32[]{:S(2)}) copy-start(f32[1024,4,128]{2,1,0:T(4,128)} %param.14) | copy-start | bytes 6291460
  35.2 62.3 %copy-start.13 = (f32[128]{0:T(128)S(1)}, f32[128]{0:T(128)}, u32[]{:S(2)}) copy-start(f32[128]{0:T(128)} %param.20) | copy-start | bytes 1540
  35.8 1.3 collective-permute-start.1
  36.4 61.0 %copy-start.10 = (s32[2]{0:T(128)S(1)}, s32[2]{0:T(128)}, u32[]{:S(2)}) copy-start(s32[2]{0:T(128)} %pad_add_fusion.place_ref) | copy-start | bytes 28
  37.2 0.7 copy-start.14
  39.7 125.0 %reduce-scatter.2.cloned.1.call-start = ((), (), s32[]{:S(2)}) async-start(), calls=%async_computation.1 | async-start | bytes 4718592 | tf_op jit(solution)/shard_map/reduce_scatter | solution.py:369
  94.1 3.3 %collective-permute-start.2 = (bf16[2,128,128]{2,1,0:T(8,128)(2,1)}, bf16[2,128,128]{2,1,0:T(8,128)(2,1)S(1)}, u32[]{:S(2)}, u32[]{:S(2)}) collective-permute-start(bf16[2,128,128]{2,1,0:T(8,128)(2,1)} %get-tuple-element.18), channel_id=1, source_target_pairs={{0,8},{8,0},{1,9},{9,1},{2,10},{10,2},{3,11},{11,3},{4,12},{12,4},... | collective-permute-start | bytes 196616 | tf_op jit(solution)/shard_map/ppermute | solution.py:367
  97.4 1.6 copy-start.3
  99.0 1.6 copy-start.5
  100.6 0.8 copy-start.8
  106.2 1.9 %copy-start = (bf16[1024,2048]{1,0:T(8,128)(2,1)}, bf16[1024,2048]{1,0:T(8,128)(2,1)S(1)}, u32[]{:S(2)}) copy-start(bf16[1024,2048]{1,0:T(8,128)(2,1)S(1)} %gated_output.1) | copy-start | bytes 12582916
Sparse Core Ops, SparseCore 0:
  39.8 51.8 all-gather.2
  108.3 56.3 reduce-scatter.1
